TPU v7x, 32 devices: a whole 2x2x4 slice. The times are simulated.
32 devices in a mesh: seq: 8 (over z, y), head: 4 (over x, core).
Axes of the slice: x: 2, y: 2, z: 4, core: 2. Of those that a mesh axis runs over, the one named last changes fastest.
Arguments:
- queries: bfloat16 [4096, 4096], P('seq', 'head'), may hold values from -5 to 5
- keys: bfloat16 [4096, 1024], P('seq', 'head'), may hold values from -5 to 5
- values: bfloat16 [4096, 1024], P('seq', 'head'), may hold values from -5 to 5
- doc_lengths: int32 [16], replicated, may hold values from 1 to 2048, 4096 in all
- out_weight: bfloat16 [4096, 4096], P('head', 'seq'), may hold values from -0.125 to 0.125
Outputs:
- mixed: bfloat16 [4096, 4096], P('seq', 'head')
Inputs may be any that keep to these rules, and one draw needn't show every extreme that they name: `doc_lengths`: the lengths sum to 4096, and one document is exactly 2048 tokens long.
All inputs are finite; a program needn't handle non-finite values.
Results may differ from a plain program's by a relative error of at most 0.012.
Values may be sent and summed in bfloat16 or wider, within the bound.
No kernel may reach another device: no remote copies, remote signals or barrier semaphores. Data moves between devices by JAX's collectives and lax.ppermute only.
A program may use at most 128 MiB of HBM per device.

v0:
```python
import functools

import jax
import jax.numpy as jnp
import numpy as np
from jax import lax
from jax.experimental import pallas as pl
from jax.experimental.layout import Layout, with_layout_constraint
from jax.experimental.pallas import tpu as pltpu
from jax.sharding import PartitionSpec as P

HQ = 32
KV = 8
DH = 128
MOST = 2048
CALLS = 1


def attend_kernel(count, heads, column, first, lengths, q_ref, *refs):
    kv_refs = refs[: 2 * count]
    o_ref, k_buf, v_buf, m_ref, l_ref, acc_ref, sems = refs[2 * count + (not first) :]
    rows = q_ref.shape[0]
    factor = float(np.log2(np.e) / np.sqrt(DH))
    s, hops = lax.axis_index("seq"), count // 2 - 1
    q_first = s * rows

    def base_of(piece):
        hop = piece - hops - 1
        odd = s % 2
        along = s - 2 * piece
        across = jnp.where(odd == 1, s - 2 * hop - 1, s - 2 * hop + 1)
        valid = (across < s) & (hop <= hops - odd)
        return jnp.where(piece <= hops, along, jnp.where(valid, across, -(1 << 12))) * rows

    q_pos = q_first + lax.broadcasted_iota(jnp.int32, (1, rows), 1)

    def one_document(i, state):
        start, first_lo, last_lo, lo = state
        first_lo = jnp.where(start <= q_first, start, first_lo)
        last_lo = jnp.where(start < q_first + rows, start, last_lo)
        return start + lengths[i], first_lo, last_lo, jnp.where(start <= q_pos, start, lo)

    zero = jnp.int32(0)
    _, first_lo, last_lo, lo = lax.fori_loop(
        0, lengths.shape[0], one_document, (zero, zero, zero, jnp.zeros((1, rows), jnp.int32))
    )

    def copies(piece, at):
        for side, buf in enumerate((k_buf, v_buf)):
            yield pltpu.make_async_copy(
                kv_refs[side * count + at].at[:, column * DH : (column + 1) * DH],
                buf.at[piece],
                sems.at[side, piece],
            )

    for piece in range(count):

        @pl.when(first_lo < base_of(piece) + rows)
        def _():
            for copy in copies(piece, piece):
                copy.start()

    half = rows // 2

    def fold(piece, head, scores, first, columns):
        top = jnp.max(scores, axis=0, keepdims=True)
        if not first:
            old = m_ref[head, :, columns]
            top = jnp.maximum(old, top)
        probs = jnp.exp2((scores - top) * factor)
        total = jnp.sum(probs, axis=0, keepdims=True)
        out = lax.dot_general(
            v_buf[piece, : probs.shape[0]],
            probs.astype(jnp.bfloat16),
            (((0,), (0,)), ((), ())),
            preferred_element_type=jnp.float32,
        )
        if not first:
            fade = jnp.exp2((old - top) * factor)
            total = l_ref[head, :, columns] * fade + total
            out = acc_ref[head, :, columns] * fade + out
        m_ref[head, :, columns] = top
        l_ref[head, :, columns] = total
        acc_ref[head, :, columns] = out

    def scores_of(piece, head, count, columns):
        return lax.dot_general(
            k_buf[piece, :count],
            q_ref[columns, head * DH : (head + 1) * DH],
            (((1,), (1,)), ((), ())),
            preferred_element_type=jnp.float32,
        )

    for copy in copies(0, 0):
        copy.wait()
    for side in range(2):
        columns, deep = slice(side * half, (side + 1) * half), (side + 1) * half
        u = lax.broadcasted_iota(jnp.int32, (deep, half), 0)
        t = side * half + lax.broadcasted_iota(jnp.int32, (deep, half), 1)
        own = (u <= t) & (u >= lo[:, columns] - q_first)
        all_scores = [scores_of(0, head, deep, columns) for head in range(heads)]
        for head in range(heads):
            fold(0, head, jnp.where(own, all_scores[head], -1e30), True, columns)

    everything = slice(0, rows)

    @pl.loop(1, count)
    def _(piece):
        base = base_of(piece)
        needed = first_lo < base + rows

        @pl.when(needed)
        def _():
            for copy in copies(piece, 0):
                copy.wait()

        @pl.when(needed & (last_lo <= base))
        def _():
            all_scores = [scores_of(piece, head, rows, everything) for head in range(heads)]
            for head in range(heads):
                fold(piece, head, all_scores[head], False, everything)

        @pl.when(needed & (last_lo > base))
        def _():
            inside = lax.broadcasted_iota(jnp.int32, (rows, rows), 0) >= lo - base
            all_scores = [scores_of(piece, head, rows, everything) for head in range(heads)]
            for head in range(heads):
                fold(piece, head, jnp.where(inside, all_scores[head], -1e30), False, everything)

    for head in range(heads):
        result = acc_ref[head] / l_ref[head]
        o_ref[:, head * DH : (head + 1) * DH] = result.T.astype(jnp.bfloat16)


def attend(lengths, queries, ks, vs, call, group, attn):
    rows, count, first = queries.shape[0], len(ks), attn is None
    anywhere = pl.BlockSpec(memory_space=pl.ANY)
    return pl.pallas_call(
        functools.partial(attend_kernel, count, group, call // CALLS, first),
        grid=(1,),
        out_shape=jax.ShapeDtypeStruct(queries.shape, jnp.bfloat16),
        in_specs=[
            pl.BlockSpec(memory_space=pltpu.SMEM),
            pl.BlockSpec((rows, group * DH), lambda i: (0, call)),
        ]
        + [anywhere] * (2 * count + (not first)),
        out_specs=pl.BlockSpec((rows, group * DH), lambda i: (0, call)),
        scratch_shapes=[
            pltpu.VMEM((count, rows, DH), jnp.bfloat16),
            pltpu.VMEM((count, rows, DH), jnp.bfloat16),
            pltpu.VMEM((group, 1, rows), jnp.float32),
            pltpu.VMEM((group, 1, rows), jnp.float32),
            pltpu.VMEM((group, DH, rows), jnp.float32),
            pltpu.SemaphoreType.DMA((2, count)),
        ],
        input_output_aliases={} if first else {2 + 2 * count: 0},
        cost_estimate=pl.CostEstimate(
            flops=4 * rows * rows * DH * group * count,
            bytes_accessed=4 * rows * DH * (group + count),
            transcendentals=rows * rows * group * count,
        ),
    )(lengths, queries, *ks, *vs, *([] if first else [attn]))


def steps(queries, keys, values, doc_lengths, out_weight):
    n, nh = lax.axis_size("seq"), lax.axis_size("head")
    rows = queries.shape[0]
    kv_local = keys.shape[1] // DH
    hops = -(-(-(-MOST // rows)) // 2)
    blocks_per_head = n // nh
    s, h = lax.axis_index("seq"), lax.axis_index("head")

    def spread(own):
        same, across = [own], []
        for hop in range(hops + 1):
            if hop > 0:
                up = [(i - 2, i) for i in range(2 * hop, n)]
                same.append(lax.ppermute(same[-1], "seq", up))
            pairs = [(i ^ 1, i) for i in range(2 * hop, n)]
            if hop == 0:
                pairs = [p for p in pairs if p[1] % 2 == 1]
            elif hop == hops:
                pairs = [p for p in pairs if p[1] % 2 == 0]
            across.append(lax.ppermute(same[-1], "seq", pairs))
        return same + across

    ks, vs = spread(keys), spread(values)

    order = list(range(0, n, 2)) + list(range(n - 1, 0, -2))
    place = {v: i for i, v in enumerate(order)}
    ahead = [(order[i], order[(i + 1) % n]) for i in range(n)]
    behind = [(b, a) for a, b in ahead]
    depth, width = out_weight.shape
    blocks = {0: [out_weight[:, : width // 2], out_weight[:, width // 2 :]]}
    forth, back = list(blocks[0]), list(blocks[0])
    for i in range(1, n // 2):
        for part in range(2):
            forth[part] = lax.ppermute(forth[part], "seq", ahead)
            back[part] = lax.ppermute(back[part], "seq", behind)
        blocks[-i], blocks[i] = list(forth), list(back)
    upper, lower = slice(0, depth // 2), slice(depth // 2, depth)
    far = [
        [lax.ppermute(forth[0], "seq", ahead)],
        [lax.ppermute(forth[1][upper], "seq", ahead), lax.ppermute(back[1][lower], "seq", behind)],
    ]

    pairs_of = [(i, i - n // 2) for i in range(1, n // 2)]
    pairs_of.sort(key=lambda p: max(p[0], -p[1]))
    pairs_of.append((0, n // 2))
    final = len(pairs_of) - 1

    def goal(i, shift):
        return order[(place[i] + shift) % n]

    def place_of(block):
        return jnp.where(block % 2 == 0, block // 2, n // 2 + (n - 1 - block) // 2)

    def head_of(shift):
        at = (place_of(s) + shift + n) % n
        return jnp.where(at < n // 2, 2 * at, 2 * (n - 1 - at) + 1) // blocks_per_head

    attn = None
    for call in range(kv_local * CALLS):
        attn = attend(doc_lengths, queries, ks, vs, call, HQ // KV // CALLS, attn)

    def times(chosen):
        at, total = 0, None
        for w in chosen:
            term = jnp.dot(attn[:, at : at + w.shape[0]], w, preferred_element_type=jnp.float32)
            total = term if total is None else total + term
            at += w.shape[0]
        return total.astype(jnp.bfloat16)

    def added(one, two):
        return (one.astype(jnp.float32) + two.astype(jnp.float32)).astype(jnp.bfloat16)

    def reduced(step, ones, twos):
        one_first = ((head_of(pairs_of[step][0]) ^ h) & 1) == 1
        swap = [(i * nh + j, i * nh + (j ^ 1)) for i in range(n) for j in range(nh)]
        sent = [times([jnp.where(one_first, a, b) for a, b in zip(x, y)]) for x, y in zip(ones, twos)]
        part = jnp.concatenate(sent, axis=1)
        arrived = lax.ppermute(part, ("seq", "head"), swap)
        kept = [times([jnp.where(one_first, b, a) for a, b in zip(x, y)]) for x, y in zip(ones, twos)]
        part = added(jnp.concatenate(kept, axis=1), arrived)
        bit = 2
        while bit < nh:
            pairs = []
            for i in range(n):
                for j in range(nh):
                    for shift in pairs_of[step]:
                        off = j ^ (goal(i, shift) // blocks_per_head)
                        if off & bit and not off & (bit - 1):
                            pairs.append((i * nh + j, i * nh + (j ^ bit)))
            arrived = lax.ppermute(part, ("seq", "head"), pairs)
            bit *= 2
            if bit < nh:
                part = added(part, arrived)
        return added(part, arrived)

    def laid(array, step, column):
        rest = blocks_per_head * width - array.shape[1]
        total = None
        for slot in range(blocks_per_head):
            ahead_by = (place_of(h * blocks_per_head + slot) - place_of(s) + n) % n
            here = (ahead_by == pairs_of[step][0] % n) | (ahead_by == pairs_of[step][1] % n)
            begin = slot * width + column
            term = jnp.where(here, array, jnp.zeros_like(array))
            term = lax.pad(term, jnp.bfloat16(0), ((0, 0, 0), (begin, rest - begin, 0)))
            total = term if total is None else total + term
        return total

    mixed = None
    for step, (one, two) in enumerate(pairs_of[:-1]):
        whole = reduced(step, [[w] for w in blocks[one]], [[w] for w in blocks[two]])
        part = laid(whole, step, 0)
        mixed = part if mixed is None else mixed + part
    left = reduced(final, [[blocks[0][0]]], [far[0]])
    mixed = with_layout_constraint(mixed + laid(left, final, 0), Layout(major_to_minor=(0, 1)))
    mixed = lax.optimization_barrier(mixed)
    right = reduced(final, [[blocks[0][1][upper], blocks[0][1][lower]]], [far[1]])
    return mixed + laid(right, final, width // 2)


def solution(mesh):
    return jax.shard_map(
        steps,
        mesh=mesh,
        in_specs=(P("seq", "head"), P("seq", "head"), P("seq", "head"), P(), P("head", "seq")),
        out_specs=P("seq", "head"),
        check_vma=False,
    )
```

profile of v0, /device:TPU:28, one launch (start us, length us, event | category | flops | bytes accessed | tf_op | source)
XLA Modules:
  0.0 166.4 jit_solution(2348709792972129765)
XLA Ops:
  0.0 1.3 collective-permute-start
  1.3 1.3 collective-permute-start.2
  2.6 1.3 collective-permute-start.7
  3.9 1.3 collective-permute-start.5
  5.2 6.0 %collective-permute-done.refs_1_ = bf16[512,256]{1,0:T(8,128)(2,1)S(1)} collective-permute-done((bf16[512,256]{1,0:T(8,128)(2,1)}, bf16[512,256]{1,0:T(8,128)(2,1)S(1)}, u32[]{:S(2)}, u32[]{:S(2)}) %collective-permute-start) | collective-permute-done | bytes 262176 | tf_op jit(solution)/shard_map/ppermute | solution.py:178
  11.2 1.9 %collective-permute-start.3 = (bf16[512,256]{1,0:T(8,128)(2,1)S(1)}, bf16[512,256]{1,0:T(8,128)(2,1)S(1)}, u32[]{:S(2)}, u32[]{:S(2)}) collective-permute-start(bf16[512,256]{1,0:T(8,128)(2,1)S(1)} %collective-permute-done.refs_1_), channel_id=1, source_target_pairs={{12,8},{8,12},{20,16},{16,20},{28,24},{24,28},{13,9},{9,13},{21,17... | collective-permute-start | bytes 786440 | tf_op jit(solution)/shard_map/ppermute | solution.py:184
  13.1 1.3 fusion.56
  14.4 1.3 collective-permute-start.1
  15.8 3.9 %collective-permute-start.8 = (bf16[512,256]{1,0:T(8,128)(2,1)S(1)}, bf16[512,256]{1,0:T(8,128)(2,1)S(1)}, u32[]{:S(2)}, u32[]{:S(2)}) collective-permute-start(bf16[512,256]{1,0:T(8,128)(2,1)S(1)} %collective-permute-done.5.refs_7_), channel_id=1, source_target_pairs={{12,8},{8,12},{20,16},{16,20},{28,24},{24,28},{13,9},{9,13},{21,17... | collective-permute-start | bytes 786440 | tf_op jit(solution)/shard_map/ppermute | solution.py:184
  19.7 0.7 copy-done.3
  20.4 2.7 %collective-permute-start.14 = (bf16[1024,256]{1,0:T(8,128)(2,1)S(1)}, bf16[1024,256]{1,0:T(8,128)(2,1)S(1)}, u32[]{:S(2)}, u32[]{:S(2)}) collective-permute-start(bf16[1024,256]{1,0:T(8,128)(2,1)S(1)} %get-tuple-element.11), channel_id=1, source_target_pairs={{0,8},{8,16},{16,24},{24,28},{28,20},{20,12},{12,4},{4,0},{1,9},{9... | collective-permute-start | bytes 1572872 | tf_op jit(solution)/shard_map/ppermute | solution.py:198
  23.1 0.7 collective-permute-done.3.refs_4_
  23.8 0.7 copy-done.6
  24.5 2.6 %collective-permute-start.10 = (bf16[1024,256]{1,0:T(8,128)(2,1)S(1)}, bf16[1024,256]{1,0:T(8,128)(2,1)S(1)}, u32[]{:S(2)}, u32[]{:S(2)}) collective-permute-start(bf16[1024,256]{1,0:T(8,128)(2,1)S(1)} %get-tuple-element.12), channel_id=1, source_target_pairs={{0,8},{8,16},{16,24},{24,28},{28,20},{20,12},{12,4},{4,0},{1,9},{9... | collective-permute-start | bytes 1572872 | tf_op jit(solution)/shard_map/ppermute | solution.py:198
  27.2 2.3 %collective-permute-done.8.refs_10_ = bf16[512,256]{1,0:T(8,128)(2,1)S(1)} collective-permute-done((bf16[512,256]{1,0:T(8,128)(2,1)S(1)}, bf16[512,256]{1,0:T(8,128)(2,1)S(1)}, u32[]{:S(2)}, u32[]{:S(2)}) %collective-permute-start.8) | collective-permute-done | bytes 262176 | tf_op jit(solution)/shard_map/ppermute | solution.py:184
  29.4 1.3 collective-permute-start.6
  30.7 20.1 %collective-permute-done.6.refs_8_ = bf16[512,256]{1,0:T(8,128)(2,1)S(1)} collective-permute-done((bf16[512,256]{1,0:T(8,128)(2,1)S(1)}, bf16[512,256]{1,0:T(8,128)(2,1)S(1)}, u32[]{:S(2)}, u32[]{:S(2)}) %collective-permute-start.6) | collective-permute-done | bytes 262176 | tf_op jit(solution)/shard_map/ppermute | solution.py:178
  50.8 4.6 %collective-permute-start.4 = (bf16[512,256]{1,0:T(8,128)(2,1)}, bf16[512,256]{1,0:T(8,128)(2,1)}, u32[]{:S(2)}, u32[]{:S(2)}) collective-permute-start(bf16[512,256]{1,0:T(8,128)(2,1)} %collective-permute-done.1.refs_2_), channel_id=1, source_target_pairs={{20,16},{28,24},{21,17},{29,25},{22,18},{30,26},{23,19},{31,27}} | collective-permute-start | bytes 786440 | tf_op jit(solution)/shard_map/ppermute | solution.py:184
  55.4 2.0 %collective-permute-start.9 = (bf16[512,256]{1,0:T(8,128)(2,1)S(1)}, bf16[512,256]{1,0:T(8,128)(2,1)}, u32[]{:S(2)}, u32[]{:S(2)}) collective-permute-start(bf16[512,256]{1,0:T(8,128)(2,1)S(1)} %collective-permute-done.6.refs_8_), channel_id=1, source_target_pairs={{20,16},{28,24},{21,17},{29,25},{22,18},{30,26},{23,19},{31,27}} | collective-permute-start | bytes 786440 | tf_op jit(solution)/shard_map/ppermute | solution.py:184
  57.4 2.0 %collective-permute-start.15 = (bf16[1024,256]{1,0:T(8,128)(2,1)S(1)}, bf16[1024,256]{1,0:T(8,128)(2,1)}, u32[]{:S(2)}, u32[]{:S(2)}) collective-permute-start(bf16[1024,256]{1,0:T(8,128)(2,1)S(1)} %collective-permute-done.14), channel_id=1, source_target_pairs={{0,8},{8,16},{16,24},{24,28},{28,20},{20,12},{12,4},{4,0},{1,9},{9... | collective-permute-start | bytes 1572872 | tf_op jit(solution)/shard_map/ppermute | solution.py:198
  59.5 2.2 %collective-permute-done.4.refs_5_ = bf16[512,256]{1,0:T(8,128)(2,1)} collective-permute-done((bf16[512,256]{1,0:T(8,128)(2,1)}, bf16[512,256]{1,0:T(8,128)(2,1)}, u32[]{:S(2)}, u32[]{:S(2)}) %collective-permute-start.4) | collective-permute-done | bytes 262176 | tf_op jit(solution)/shard_map/ppermute | solution.py:184
  61.7 5.5 %collective-permute-done.9.refs_11_ = bf16[512,256]{1,0:T(8,128)(2,1)} collective-permute-done((bf16[512,256]{1,0:T(8,128)(2,1)S(1)}, bf16[512,256]{1,0:T(8,128)(2,1)}, u32[]{:S(2)}, u32[]{:S(2)}) %collective-permute-start.9) | collective-permute-done | bytes 262176 | tf_op jit(solution)/shard_map/ppermute | solution.py:184
  67.2 13.2 %shard_map.55.refs_12_ = bf16[512,1024]{1,0:T(8,128)(2,1)} custom-call(s32[16]{0:T(128)} %lengths.3, bf16[512,1024]{1,0:T(8,128)(2,1)} %q_ref.3, bf16[512,256]{1,0:T(8,128)(2,1)} %refs_0_.3, bf16[512,256]{1,0:T(8,128)(2,1)} %copy-done.2, bf16[512,256]{1,0:T(8,128)(2,1)} %collective-permute-done.1.refs_2_, bf16[512,256]{1,0:T(8,128)(2,1)} %copy-done.3, ...), custom_call_target="tpu_custom_call" | custom-call | flops 3221225472 | bytes 2621440 | tf_op jit(solution)/shard_map/pallas_call | solution.py:138
  80.5 13.3 %shard_map.56 = bf16[512,1024]{1,0:T(8,128)(2,1)} custom-call(s32[16]{0:T(128)} %lengths.3, bf16[512,1024]{1,0:T(8,128)(2,1)} %q_ref.3, bf16[512,256]{1,0:T(8,128)(2,1)} %refs_0_.3, bf16[512,256]{1,0:T(8,128)(2,1)} %copy-done.2, bf16[512,256]{1,0:T(8,128)(2,1)} %collective-permute-done.1.refs_2_, ...), custom_call_target="tpu_custom_call", output_to_operand_aliasing={{}: (14, {})} | custom-call | flops 3221225472 | bytes 2621440 | tf_op jit(solution)/shard_map/pallas_call | solution.py:138
  93.8 1.9 %convolution_convert_fusion.10 = bf16[512,256]{1,0:T(8,128)(2,1)S(1)} fusion(bf16[512,1024]{1,0:T(8,128)(2,1)} %shard_map.56, bf16[1024,256]{1,0:T(8,128)(2,1)} %collective-permute-done.17, bf16[1024,256]{1,0:T(8,128)(2,1)} %collective-permute-done.15, pred[]{:T(512)S(6)} %eq.141), kind=kOutput, calls=%fused_computation.20 | convolution fusion | flops 268828672 | bytes 2359297 | tf_op jit(solution)/shard_map/dot_general | solution.py:229
  95.7 0.4 convolution_convert_fusion.11
  96.3 2.0 %collective-permute-start.21 = (bf16[1024,256]{1,0:T(8,128)(2,1)}, bf16[1024,256]{1,0:T(8,128)(2,1)S(1)}, u32[]{:S(2)}, u32[]{:S(2)}) collective-permute-start(bf16[1024,256]{1,0:T(8,128)(2,1)} %collective-permute-done.15), channel_id=1, source_target_pairs={{0,8},{8,16},{16,24},{24,28},{28,20},{20,12},{12,4},{4,0},{1,9},{9... | collective-permute-start | bytes 1572872 | tf_op jit(solution)/shard_map/ppermute | solution.py:198
  98.4 2.0 %collective-permute-start.20 = (bf16[1024,256]{1,0:T(8,128)(2,1)S(1)}, bf16[1024,256]{1,0:T(8,128)(2,1)S(1)}, u32[]{:S(2)}, u32[]{:S(2)}) collective-permute-start(bf16[1024,256]{1,0:T(8,128)(2,1)S(1)} %collective-permute-done.11), channel_id=1, source_target_pairs={{0,8},{8,16},{16,24},{24,28},{28,20},{20,12},{12,4},{4,0},{1,9},{9... | collective-permute-start | bytes 1572872 | tf_op jit(solution)/shard_map/ppermute | solution.py:198
  100.4 1.5 convolution_convert_fusion.12
  101.9 0.4 convolution_convert_fusion.13
  102.3 9.0 %collective-permute-done.25 = bf16[1024,256]{1,0:T(8,128)(2,1)S(1)} collective-permute-done((bf16[1024,256]{1,0:T(8,128)(2,1)}, bf16[1024,256]{1,0:T(8,128)(2,1)S(1)}, u32[]{:S(2)}, u32[]{:S(2)}) %collective-permute-start.25) | collective-permute-done | bytes 524320 | tf_op jit(solution)/shard_map/ppermute | solution.py:199
  111.4 0.2 collective-permute-start.32
  111.6 2.1 %collective-permute-start.31 = (bf16[512,256]{1,0:T(8,128)(2,1)S(1)}, bf16[512,256]{1,0:T(8,128)(2,1)S(1)}, u32[]{:S(2)}, u32[]{:S(2)}) collective-permute-start(bf16[512,256]{1,0:T(8,128)(2,1)S(1)} %slice.37), channel_id=1, source_target_pairs={{0,8},{8,16},{16,24},{24,28},{28,20},{20,12},{12,4},{4,0},{1,9},{9... | collective-permute-start | bytes 786440 | tf_op jit(solution)/shard_map/ppermute | solution.py:204
  113.7 0.4 convolution_convert_fusion.2
  114.1 8.4 %collective-permute-done.24 = bf16[1024,256]{1,0:T(8,128)(2,1)S(1)} collective-permute-done((bf16[1024,256]{1,0:T(8,128)(2,1)S(1)}, bf16[1024,256]{1,0:T(8,128)(2,1)S(1)}, u32[]{:S(2)}, u32[]{:S(2)}) %collective-permute-start.24) | collective-permute-done | bytes 524320 | tf_op jit(solution)/shard_map/ppermute | solution.py:199
  122.6 0.4 convolution_convert_fusion.3
  123.3 3.4 %collective-permute-start.19 = (bf16[512,512]{1,0:T(8,128)(2,1)S(1)}, bf16[512,512]{1,0:T(8,128)(2,1)S(1)}, u32[]{:S(2)}, u32[]{:S(2)}) collective-permute-start(bf16[512,512]{1,0:T(8,128)(2,1)S(1)} %add_convert_fusion.5), channel_id=1, source_target_pairs={{0,2},{3,1},{4,6},{7,5},{9,11},{10,8},{13,15},{14,12},{17,19},{18,... | collective-permute-start | bytes 1572872 | tf_op jit(solution)/shard_map/ppermute | solution.py:254
  126.7 0.4 convolution_convert_fusion.6
  127.2 0.4 convolution_convert_fusion.7
  127.8 0.4 convolution_convert_fusion.4
  128.2 0.4 convolution_convert_fusion.8
  128.7 0.4 convolution_convert_fusion.5
  129.1 0.4 convolution_convert_fusion.9
  129.7 0.7 copy-done
  130.4 0.3 fusion.36
  130.7 0.3 fusion.4
  131.0 0.6 collective-permute-start.33
  131.6 0.3 fusion.38
  131.9 0.9 collective-permute-done.33
  132.7 0.3 fusion.3
  133.0 1.3 collective-permute-start.34
  134.3 9.7 %collective-permute-done.28 = bf16[1024,256]{1,0:T(8,128)(2,1)S(1)} collective-permute-done((bf16[1024,256]{1,0:T(8,128)(2,1)S(1)}, bf16[1024,256]{1,0:T(8,128)(2,1)S(1)}, u32[]{:S(2)}, u32[]{:S(2)}) %collective-permute-start.28) | collective-permute-done | bytes 524320 | tf_op jit(solution)/shard_map/ppermute | solution.py:203
  144.0 0.4 convolution_convert_fusion
  144.7 1.3 collective-permute-start.27
  146.0 0.1 add_convert_fusion.3
  146.1 4.6 %collective-permute-start.23 = (bf16[512,512]{1,0:T(8,128)(2,1)S(1)}, bf16[512,512]{1,0:T(8,128)(2,1)S(1)}, u32[]{:S(2)}, u32[]{:S(2)}) collective-permute-start(bf16[512,512]{1,0:T(8,128)(2,1)S(1)} %add_convert_fusion.3), channel_id=1, source_target_pairs={{0,2},{3,1},{5,7},{6,4},{8,10},{11,9},{13,15},{14,12},{17,19},{18,... | collective-permute-start | bytes 1572872 | tf_op jit(solution)/shard_map/ppermute | solution.py:254
  150.7 0.4 fusion.7
  151.2 1.3 collective-permute-start.30
  152.5 0.2 broadcast_select_fusion.5
  152.8 11.3 %collective-permute-done.30 = bf16[512,256]{1,0:T(8,128)(2,1)S(1)} collective-permute-done((bf16[512,256]{1,0:T(8,128)(2,1)S(1)}, bf16[512,256]{1,0:T(8,128)(2,1)S(1)}, u32[]{:S(2)}, u32[]{:S(2)}) %collective-permute-start.30) | collective-permute-done | bytes 262176 | tf_op jit(solution)/shard_map/ppermute | solution.py:254
  164.3 0.2 broadcast_select_fusion.1
  164.5 0.2 broadcast_select_fusion.3
  164.7 0.5 add_add_fusion.1
  165.2 1.2 add_add_fusion
  (60 shorter events, 1.3 us)
Async XLA Ops:
  0.0 11.2 %collective-permute-start = (bf16[512,256]{1,0:T(8,128)(2,1)}, bf16[512,256]{1,0:T(8,128)(2,1)S(1)}, u32[]{:S(2)}, u32[]{:S(2)}) collective-permute-start(bf16[512,256]{1,0:T(8,128)(2,1)} %refs_0_.3), channel_id=1, source_target_pairs={{0,8},{4,12},{8,16},{12,20},{16,24},{20,28},{1,9},{5,13},{9,17},{1... | collective-permute-start | bytes 786440 | tf_op jit(solution)/shard_map/ppermute | solution.py:178
  1.3 18.4 %collective-permute-start.2 = (bf16[512,256]{1,0:T(8,128)(2,1)}, bf16[512,256]{1,0:T(8,128)(2,1)S(1)}, u32[]{:S(2)}, u32[]{:S(2)}) collective-permute-start(bf16[512,256]{1,0:T(8,128)(2,1)} %refs_0_.3), channel_id=1, source_target_pairs={{0,4},{8,12},{16,20},{24,28},{1,5},{9,13},{17,21},{25,29},{2,6},{1... | collective-permute-start | bytes 786440 | tf_op jit(solution)/shard_map/ppermute | solution.py:184
  2.6 17.8 %collective-permute-start.7 = (bf16[512,256]{1,0:T(8,128)(2,1)}, bf16[512,256]{1,0:T(8,128)(2,1)S(1)}, u32[]{:S(2)}, u32[]{:S(2)}) collective-permute-start(bf16[512,256]{1,0:T(8,128)(2,1)} %refs_6_.3), channel_id=1, source_target_pairs={{0,4},{8,12},{16,20},{24,28},{1,5},{9,13},{17,21},{25,29},{2,6},{1... | collective-permute-start | bytes 786440 | tf_op jit(solution)/shard_map/ppermute | solution.py:184
  3.9 11.9 %collective-permute-start.5 = (bf16[512,256]{1,0:T(8,128)(2,1)}, bf16[512,256]{1,0:T(8,128)(2,1)S(1)}, u32[]{:S(2)}, u32[]{:S(2)}) collective-permute-start(bf16[512,256]{1,0:T(8,128)(2,1)} %refs_6_.3), channel_id=1, source_target_pairs={{0,8},{4,12},{8,16},{12,20},{16,24},{20,28},{1,9},{5,13},{9,17},{1... | collective-permute-start | bytes 786440 | tf_op jit(solution)/shard_map/ppermute | solution.py:178
  11.2 3.2 %copy-start.2 = (bf16[512,256]{1,0:T(8,128)(2,1)}, bf16[512,256]{1,0:T(8,128)(2,1)S(1)}, u32[]{:S(2)}) copy-start(bf16[512,256]{1,0:T(8,128)(2,1)S(1)} %collective-permute-done.refs_1_) | copy-start | bytes 786436
  11.2 12.6 %collective-permute-start.3 = (bf16[512,256]{1,0:T(8,128)(2,1)S(1)}, bf16[512,256]{1,0:T(8,128)(2,1)S(1)}, u32[]{:S(2)}, u32[]{:S(2)}) collective-permute-start(bf16[512,256]{1,0:T(8,128)(2,1)S(1)} %collective-permute-done.refs_1_), channel_id=1, source_target_pairs={{12,8},{8,12},{20,16},{16,20},{28,24},{24,28},{13,9},{9,13},{21,17... | collective-permute-start | bytes 786440 | tf_op jit(solution)/shard_map/ppermute | solution.py:184
  14.4 10.1 %collective-permute-start.1 = (bf16[512,256]{1,0:T(8,128)(2,1)S(1)}, bf16[512,256]{1,0:T(8,128)(2,1)}, u32[]{:S(2)}, u32[]{:S(2)}) collective-permute-start(bf16[512,256]{1,0:T(8,128)(2,1)S(1)} %collective-permute-done.refs_1_), channel_id=1, source_target_pairs={{8,16},{12,20},{16,24},{20,28},{9,17},{13,21},{17,25},{21,29},{10,... | collective-permute-start | bytes 786440 | tf_op jit(solution)/shard_map/ppermute | solution.py:178
  15.8 39.7 %copy-start.5 = (bf16[512,256]{1,0:T(8,128)(2,1)}, bf16[512,256]{1,0:T(8,128)(2,1)S(1)}, u32[]{:S(2)}) copy-start(bf16[512,256]{1,0:T(8,128)(2,1)S(1)} %collective-permute-done.5.refs_7_) | copy-start | bytes 786436
  15.8 13.7 %collective-permute-start.8 = (bf16[512,256]{1,0:T(8,128)(2,1)S(1)}, bf16[512,256]{1,0:T(8,128)(2,1)S(1)}, u32[]{:S(2)}, u32[]{:S(2)}) collective-permute-start(bf16[512,256]{1,0:T(8,128)(2,1)S(1)} %collective-permute-done.5.refs_7_), channel_id=1, source_target_pairs={{12,8},{8,12},{20,16},{16,20},{28,24},{24,28},{13,9},{9,13},{21,17... | collective-permute-start | bytes 786440 | tf_op jit(solution)/shard_map/ppermute | solution.py:184
  19.7 0.7 copy-start.3
  20.4 35.0 %collective-permute-start.16 = (bf16[1024,256]{1,0:T(8,128)(2,1)S(1)}, bf16[1024,256]{1,0:T(8,128)(2,1)S(1)}, u32[]{:S(2)}, u32[]{:S(2)}) collective-permute-start(bf16[1024,256]{1,0:T(8,128)(2,1)S(1)} %get-tuple-element.11), channel_id=1, source_target_pairs={{8,0},{16,8},{24,16},{28,24},{20,28},{12,20},{4,12},{0,4},{9,1},{1... | collective-permute-start | bytes 1572872 | tf_op jit(solution)/shard_map/ppermute | solution.py:199
  20.4 3.4 %copy-start.4 = (bf16[512,256]{1,0:T(8,128)(2,1)}, bf16[512,256]{1,0:T(8,128)(2,1)S(1)}, u32[]{:S(2)}) copy-start(bf16[512,256]{1,0:T(8,128)(2,1)S(1)} %collective-permute-done.7.refs_9_) | copy-start | bytes 786436
  20.4 37.0 %collective-permute-start.14 = (bf16[1024,256]{1,0:T(8,128)(2,1)S(1)}, bf16[1024,256]{1,0:T(8,128)(2,1)S(1)}, u32[]{:S(2)}, u32[]{:S(2)}) collective-permute-start(bf16[1024,256]{1,0:T(8,128)(2,1)S(1)} %get-tuple-element.11), channel_id=1, source_target_pairs={{0,8},{8,16},{16,24},{24,28},{28,20},{20,12},{12,4},{4,0},{1,9},{9... | collective-permute-start | bytes 1572872 | tf_op jit(solution)/shard_map/ppermute | solution.py:198
  23.8 0.7 copy-start.6
  24.5 32.9 %collective-permute-start.12 = (bf16[1024,256]{1,0:T(8,128)(2,1)S(1)}, bf16[1024,256]{1,0:T(8,128)(2,1)S(1)}, u32[]{:S(2)}, u32[]{:S(2)}) collective-permute-start(bf16[1024,256]{1,0:T(8,128)(2,1)S(1)} %get-tuple-element.12), channel_id=1, source_target_pairs={{8,0},{16,8},{24,16},{28,24},{20,28},{12,20},{4,12},{0,4},{9,1},{1... | collective-permute-start | bytes 1572872 | tf_op jit(solution)/shard_map/ppermute | solution.py:199
  24.5 34.9 %collective-permute-start.10 = (bf16[1024,256]{1,0:T(8,128)(2,1)S(1)}, bf16[1024,256]{1,0:T(8,128)(2,1)S(1)}, u32[]{:S(2)}, u32[]{:S(2)}) collective-permute-start(bf16[1024,256]{1,0:T(8,128)(2,1)S(1)} %get-tuple-element.12), channel_id=1, source_target_pairs={{0,8},{8,16},{16,24},{24,28},{28,20},{20,12},{12,4},{4,0},{1,9},{9... | collective-permute-start | bytes 1572872 | tf_op jit(solution)/shard_map/ppermute | solution.py:198
  29.4 28.0 %copy-start.7 = (bf16[512,256]{1,0:T(8,128)(2,1)}, bf16[512,256]{1,0:T(8,128)(2,1)S(1)}, u32[]{:S(2)}) copy-start(bf16[512,256]{1,0:T(8,128)(2,1)S(1)} %collective-permute-done.8.refs_10_) | copy-start | bytes 786436
  29.4 21.4 %collective-permute-start.6 = (bf16[512,256]{1,0:T(8,128)(2,1)S(1)}, bf16[512,256]{1,0:T(8,128)(2,1)S(1)}, u32[]{:S(2)}, u32[]{:S(2)}) collective-permute-start(bf16[512,256]{1,0:T(8,128)(2,1)S(1)} %collective-permute-done.5.refs_7_), channel_id=1, source_target_pairs={{8,16},{12,20},{16,24},{20,28},{9,17},{13,21},{17,25},{21,29},{10,... | collective-permute-start | bytes 786440 | tf_op jit(solution)/shard_map/ppermute | solution.py:178
  50.8 16.4 %copy-start.8 = (bf16[512,256]{1,0:T(8,128)(2,1)}, bf16[512,256]{1,0:T(8,128)(2,1)S(1)}, u32[]{:S(2)}) copy-start(bf16[512,256]{1,0:T(8,128)(2,1)S(1)} %collective-permute-done.6.refs_8_) | copy-start | bytes 786436
  50.8 10.9 %collective-permute-start.4 = (bf16[512,256]{1,0:T(8,128)(2,1)}, bf16[512,256]{1,0:T(8,128)(2,1)}, u32[]{:S(2)}, u32[]{:S(2)}) collective-permute-start(bf16[512,256]{1,0:T(8,128)(2,1)} %collective-permute-done.1.refs_2_), channel_id=1, source_target_pairs={{20,16},{28,24},{21,17},{29,25},{22,18},{30,26},{23,19},{31,27}} | collective-permute-start | bytes 786440 | tf_op jit(solution)/shard_map/ppermute | solution.py:184
  55.4 11.8 %collective-permute-start.9 = (bf16[512,256]{1,0:T(8,128)(2,1)S(1)}, bf16[512,256]{1,0:T(8,128)(2,1)}, u32[]{:S(2)}, u32[]{:S(2)}) collective-permute-start(bf16[512,256]{1,0:T(8,128)(2,1)S(1)} %collective-permute-done.6.refs_8_), channel_id=1, source_target_pairs={{20,16},{28,24},{21,17},{29,25},{22,18},{30,26},{23,19},{31,27}} | collective-permute-start | bytes 786440 | tf_op jit(solution)/shard_map/ppermute | solution.py:184
  57.4 36.3 %collective-permute-start.17 = (bf16[1024,256]{1,0:T(8,128)(2,1)S(1)}, bf16[1024,256]{1,0:T(8,128)(2,1)}, u32[]{:S(2)}, u32[]{:S(2)}) collective-permute-start(bf16[1024,256]{1,0:T(8,128)(2,1)S(1)} %collective-permute-done.16), channel_id=1, source_target_pairs={{8,0},{16,8},{24,16},{28,24},{20,28},{12,20},{4,12},{0,4},{9,1},{1... | collective-permute-start | bytes 1572872 | tf_op jit(solution)/shard_map/ppermute | solution.py:199
  57.4 36.3 %collective-permute-start.15 = (bf16[1024,256]{1,0:T(8,128)(2,1)S(1)}, bf16[1024,256]{1,0:T(8,128)(2,1)}, u32[]{:S(2)}, u32[]{:S(2)}) collective-permute-start(bf16[1024,256]{1,0:T(8,128)(2,1)S(1)} %collective-permute-done.14), channel_id=1, source_target_pairs={{0,8},{8,16},{16,24},{24,28},{28,20},{20,12},{12,4},{4,0},{1,9},{9... | collective-permute-start | bytes 1572872 | tf_op jit(solution)/shard_map/ppermute | solution.py:198
  59.5 36.2 %collective-permute-start.13 = (bf16[1024,256]{1,0:T(8,128)(2,1)S(1)}, bf16[1024,256]{1,0:T(8,128)(2,1)S(1)}, u32[]{:S(2)}, u32[]{:S(2)}) collective-permute-start(bf16[1024,256]{1,0:T(8,128)(2,1)S(1)} %collective-permute-done.12), channel_id=1, source_target_pairs={{8,0},{16,8},{24,16},{28,24},{20,28},{12,20},{4,12},{0,4},{9,1},{1... | collective-permute-start | bytes 1572872 | tf_op jit(solution)/shard_map/ppermute | solution.py:199
  61.7 34.0 %collective-permute-start.11 = (bf16[1024,256]{1,0:T(8,128)(2,1)S(1)}, bf16[1024,256]{1,0:T(8,128)(2,1)S(1)}, u32[]{:S(2)}, u32[]{:S(2)}) collective-permute-start(bf16[1024,256]{1,0:T(8,128)(2,1)S(1)} %collective-permute-done.10), channel_id=1, source_target_pairs={{0,8},{8,16},{16,24},{24,28},{28,20},{20,12},{12,4},{4,0},{1,9},{9... | collective-permute-start | bytes 1572872 | tf_op jit(solution)/shard_map/ppermute | solution.py:198
  93.8 1.9 %copy-start.1 = (bf16[512,1024]{1,0:T(8,128)(2,1)S(1)}, bf16[512,1024]{1,0:T(8,128)(2,1)}, u32[]{:S(2)}) copy-start(bf16[512,1024]{1,0:T(8,128)(2,1)} %shard_map.56) | copy-start | bytes 3145732
  96.2 26.9 %collective-permute-start.18 = (bf16[512,512]{1,0:T(8,128)(2,1)S(1)}, bf16[512,512]{1,0:T(8,128)(2,1)S(1)}, u32[]{:S(2)}, u32[]{:S(2)}) collective-permute-start(bf16[512,512]{1,0:T(8,128)(2,1)S(1)} %pad_maximum_fusion), channel_id=1, source_target_pairs={{0,1},{1,0},{2,3},{3,2},{4,5},{5,4},{6,7},{7,6},{8,9},{9,8},{10,11... | collective-permute-start | bytes 1572872 | tf_op jit(solution)/shard_map/ppermute | solution.py:242
  96.3 15.1 %collective-permute-start.25 = (bf16[1024,256]{1,0:T(8,128)(2,1)}, bf16[1024,256]{1,0:T(8,128)(2,1)S(1)}, u32[]{:S(2)}, u32[]{:S(2)}) collective-permute-start(bf16[1024,256]{1,0:T(8,128)(2,1)} %collective-permute-done.17), channel_id=1, source_target_pairs={{8,0},{16,8},{24,16},{28,24},{20,28},{12,20},{4,12},{0,4},{9,1},{1... | collective-permute-start | bytes 1572872 | tf_op jit(solution)/shard_map/ppermute | solution.py:199
  96.3 15.3 %collective-permute-start.21 = (bf16[1024,256]{1,0:T(8,128)(2,1)}, bf16[1024,256]{1,0:T(8,128)(2,1)S(1)}, u32[]{:S(2)}, u32[]{:S(2)}) collective-permute-start(bf16[1024,256]{1,0:T(8,128)(2,1)} %collective-permute-done.15), channel_id=1, source_target_pairs={{0,8},{8,16},{16,24},{24,28},{28,20},{20,12},{12,4},{4,0},{1,9},{9... | collective-permute-start | bytes 1572872 | tf_op jit(solution)/shard_map/ppermute | solution.py:198
  98.4 24.2 %collective-permute-start.24 = (bf16[1024,256]{1,0:T(8,128)(2,1)S(1)}, bf16[1024,256]{1,0:T(8,128)(2,1)S(1)}, u32[]{:S(2)}, u32[]{:S(2)}) collective-permute-start(bf16[1024,256]{1,0:T(8,128)(2,1)S(1)} %collective-permute-done.13), channel_id=1, source_target_pairs={{8,0},{16,8},{24,16},{28,24},{20,28},{12,20},{4,12},{0,4},{9,1},{1... | collective-permute-start | bytes 1572872 | tf_op jit(solution)/shard_map/ppermute | solution.py:199
  98.4 28.8 %collective-permute-start.20 = (bf16[1024,256]{1,0:T(8,128)(2,1)S(1)}, bf16[1024,256]{1,0:T(8,128)(2,1)S(1)}, u32[]{:S(2)}, u32[]{:S(2)}) collective-permute-start(bf16[1024,256]{1,0:T(8,128)(2,1)S(1)} %collective-permute-done.11), channel_id=1, source_target_pairs={{0,8},{8,16},{16,24},{24,28},{28,20},{20,12},{12,4},{4,0},{1,9},{9... | collective-permute-start | bytes 1572872 | tf_op jit(solution)/shard_map/ppermute | solution.py:198
  111.4 18.2 %collective-permute-start.32 = (bf16[512,256]{1,0:T(8,128)(2,1)S(1)}, bf16[512,256]{1,0:T(8,128)(2,1)S(1)}, u32[]{:S(2)}, u32[]{:S(2)}) collective-permute-start(bf16[512,256]{1,0:T(8,128)(2,1)S(1)} %slice.39), channel_id=1, source_target_pairs={{8,0},{16,8},{24,16},{28,24},{20,28},{12,20},{4,12},{0,4},{9,1},{1... | collective-permute-start | bytes 786440 | tf_op jit(solution)/shard_map/ppermute | solution.py:204
  111.6 19.0 %collective-permute-start.31 = (bf16[512,256]{1,0:T(8,128)(2,1)S(1)}, bf16[512,256]{1,0:T(8,128)(2,1)S(1)}, u32[]{:S(2)}, u32[]{:S(2)}) collective-permute-start(bf16[512,256]{1,0:T(8,128)(2,1)S(1)} %slice.37), channel_id=1, source_target_pairs={{0,8},{8,16},{16,24},{24,28},{28,20},{20,12},{12,4},{4,0},{1,9},{9... | collective-permute-start | bytes 786440 | tf_op jit(solution)/shard_map/ppermute | solution.py:204
  123.1 21.4 %collective-permute-start.26 = (bf16[512,512]{1,0:T(8,128)(2,1)S(1)}, bf16[512,512]{1,0:T(8,128)(2,1)S(1)}, u32[]{:S(2)}, u32[]{:S(2)}) collective-permute-start(bf16[512,512]{1,0:T(8,128)(2,1)S(1)} %pad_maximum_fusion.2), channel_id=1, source_target_pairs={{0,1},{1,0},{2,3},{3,2},{4,5},{5,4},{6,7},{7,6},{8,9},{9,8},{10,11... | collective-permute-start | bytes 1572872 | tf_op jit(solution)/shard_map/ppermute | solution.py:242
  123.3 29.2 %collective-permute-start.19 = (bf16[512,512]{1,0:T(8,128)(2,1)S(1)}, bf16[512,512]{1,0:T(8,128)(2,1)S(1)}, u32[]{:S(2)}, u32[]{:S(2)}) collective-permute-start(bf16[512,512]{1,0:T(8,128)(2,1)S(1)} %add_convert_fusion.5), channel_id=1, source_target_pairs={{0,2},{3,1},{4,6},{7,5},{9,11},{10,8},{13,15},{14,12},{17,19},{18,... | collective-permute-start | bytes 1572872 | tf_op jit(solution)/shard_map/ppermute | solution.py:254
  127.7 18.3 %collective-permute-start.22 = (bf16[512,512]{1,0:T(8,128)(2,1)S(1)}, bf16[512,512]{1,0:T(8,128)(2,1)S(1)}, u32[]{:S(2)}, u32[]{:S(2)}) collective-permute-start(bf16[512,512]{1,0:T(8,128)(2,1)S(1)} %pad_maximum_fusion.1), channel_id=1, source_target_pairs={{0,1},{1,0},{2,3},{3,2},{4,5},{5,4},{6,7},{7,6},{8,9},{9,8},{10,11... | collective-permute-start | bytes 1572872 | tf_op jit(solution)/shard_map/ppermute | solution.py:242
  129.1 1.2 copy-start
  129.6 14.4 %collective-permute-start.28 = (bf16[1024,256]{1,0:T(8,128)(2,1)S(1)}, bf16[1024,256]{1,0:T(8,128)(2,1)S(1)}, u32[]{:S(2)}, u32[]{:S(2)}) collective-permute-start(bf16[1024,256]{1,0:T(8,128)(2,1)S(1)} %collective-permute-done.20), channel_id=1, source_target_pairs={{0,8},{8,16},{16,24},{24,28},{28,20},{20,12},{12,4},{4,0},{1,9},{9... | collective-permute-start | bytes 1572872 | tf_op jit(solution)/shard_map/ppermute | solution.py:203
  131.0 1.7 %collective-permute-start.33 = (bf16[512,256]{1,0:T(8,128)(2,1)S(1)}, bf16[512,256]{1,0:T(8,128)(2,1)S(1)}, u32[]{:S(2)}, u32[]{:S(2)}) collective-permute-start(bf16[512,256]{1,0:T(8,128)(2,1)S(1)} %fusion.4), channel_id=1, source_target_pairs={{0,1},{1,0},{2,3},{3,2},{4,5},{5,4},{6,7},{7,6},{8,9},{9,8},{10,11... | collective-permute-start | bytes 786440 | tf_op jit(solution)/shard_map/ppermute | solution.py:242
  133.0 19.7 %collective-permute-start.34 = (bf16[512,256]{1,0:T(8,128)(2,1)S(1)}, bf16[512,256]{1,0:T(8,128)(2,1)S(1)}, u32[]{:S(2)}, u32[]{:S(2)}) collective-permute-start(bf16[512,256]{1,0:T(8,128)(2,1)S(1)} %fusion.3), channel_id=1, source_target_pairs={{1,3},{2,0},{5,7},{6,4},{8,10},{11,9},{12,14},{15,13},{16,18},{19,... | collective-permute-start | bytes 786440 | tf_op jit(solution)/shard_map/ppermute | solution.py:254
  144.4 6.3 %collective-permute-start.29 = (bf16[512,256]{1,0:T(8,128)(2,1)S(1)}, bf16[512,256]{1,0:T(8,128)(2,1)S(1)}, u32[]{:S(2)}, u32[]{:S(2)}) collective-permute-start(bf16[512,256]{1,0:T(8,128)(2,1)S(1)} %convolution_convert_fusion), channel_id=1, source_target_pairs={{0,1},{1,0},{2,3},{3,2},{4,5},{5,4},{6,7},{7,6},{8,9},{9,8},{10,11... | collective-permute-start | bytes 786440 | tf_op jit(solution)/shard_map/ppermute | solution.py:242
  144.7 19.6 %collective-permute-start.27 = (bf16[512,512]{1,0:T(8,128)(2,1)S(1)}, bf16[512,512]{1,0:T(8,128)(2,1)S(1)}, u32[]{:S(2)}, u32[]{:S(2)}) collective-permute-start(bf16[512,512]{1,0:T(8,128)(2,1)S(1)} %add_convert_fusion.1), channel_id=1, source_target_pairs={{1,3},{2,0},{4,6},{7,5},{9,11},{10,8},{12,14},{15,13},{16,18},{19,... | collective-permute-start | bytes 1572872 | tf_op jit(solution)/shard_map/ppermute | solution.py:254
  146.1 18.4 %collective-permute-start.23 = (bf16[512,512]{1,0:T(8,128)(2,1)S(1)}, bf16[512,512]{1,0:T(8,128)(2,1)S(1)}, u32[]{:S(2)}, u32[]{:S(2)}) collective-permute-start(bf16[512,512]{1,0:T(8,128)(2,1)S(1)} %add_convert_fusion.3), channel_id=1, source_target_pairs={{0,2},{3,1},{5,7},{6,4},{8,10},{11,9},{13,15},{14,12},{17,19},{18,... | collective-permute-start | bytes 1572872 | tf_op jit(solution)/shard_map/ppermute | solution.py:254
  151.2 13.0 %collective-permute-start.30 = (bf16[512,256]{1,0:T(8,128)(2,1)S(1)}, bf16[512,256]{1,0:T(8,128)(2,1)S(1)}, u32[]{:S(2)}, u32[]{:S(2)}) collective-permute-start(bf16[512,256]{1,0:T(8,128)(2,1)S(1)} %fusion.7), channel_id=1, source_target_pairs={{1,3},{2,0},{5,7},{6,4},{8,10},{11,9},{12,14},{15,13},{16,18},{19,... | collective-permute-start | bytes 786440 | tf_op jit(solution)/shard_map/ppermute | solution.py:254
where the time goes:
time: 167 us; the launch traced here: 166 us
  waiting for transfers between devices  76.1 us (46%)
  starting transfers between devices  46.8 us (28%)
  Pallas kernels  26.5 us (16%)
  matrix products  9.93 us (6%)
  local copies, waits for them, and re-layouts  3.44 us (2%)
  other arithmetic  3 us (2%)
    pallas_call x2, Pallas kernels, attend(): pl.pallas_call(functools.partial(attend_kernel, count, group, call // CAL...  26.5 us
    ppermute x4, waiting for transfers between devices, spread(): same.append(lax.ppermute(same[-1], 'seq', up))  26.2 us
    ppermute x6, waiting for transfers between devices, steps(): back[part] = lax.ppermute(back[part], 'seq', behind)  17.4 us
    ppermute x6, starting transfers between devices, spread(): across.append(lax.ppermute(same[-1], 'seq', pairs))  15 us
    ppermute x5, starting transfers between devices, reduced(): arrived = lax.ppermute(part, ('seq', 'head'), pairs)  11.9 us
    ppermute x5, waiting for transfers between devices, reduced(): arrived = lax.ppermute(part, ('seq', 'head'), pairs)  11.3 us
    ppermute x6, starting transfers between devices, steps(): forth[part] = lax.ppermute(forth[part], 'seq', ahead)  11.3 us
    ppermute x6, waiting for transfers between devices, spread(): across.append(lax.ppermute(same[-1], 'seq', pairs))  10.6 us
  transfers between devices with their start and end apart: 35, of which 11 were waited for; matrix products, arithmetic and copies ran while one was open for 7% of the time, Pallas kernels for 16%

commit v1 on v0

--- a/solution.py
+++ b/solution.py
@@ -62,7 +62,7 @@
 
     half = rows // 2
 
-    def fold(piece, head, scores, first, columns):
+    def fold(piece, head, scores, first, columns, begin=0):
         top = jnp.max(scores, axis=0, keepdims=True)
         if not first:
             old = m_ref[head, :, columns]
@@ -70,7 +70,7 @@
         probs = jnp.exp2((scores - top) * factor)
         total = jnp.sum(probs, axis=0, keepdims=True)
         out = lax.dot_general(
-            v_buf[piece, : probs.shape[0]],
+            v_buf[piece, begin : begin + probs.shape[0]],
             probs.astype(jnp.bfloat16),
             (((0,), (0,)), ((), ())),
             preferred_element_type=jnp.float32,
@@ -83,9 +83,9 @@
         l_ref[head, :, columns] = total
         acc_ref[head, :, columns] = out
 
-    def scores_of(piece, head, count, columns):
+    def scores_of(piece, head, count, columns, begin=0):
         return lax.dot_general(
-            k_buf[piece, :count],
+            k_buf[piece, begin : begin + count],
             q_ref[columns, head * DH : (head + 1) * DH],
             (((1,), (1,)), ((), ())),
             preferred_element_type=jnp.float32,
@@ -120,12 +120,16 @@
             for head in range(heads):
                 fold(piece, head, all_scores[head], False, everything)
 
-        @pl.when(needed & (last_lo > base))
-        def _():
-            inside = lax.broadcasted_iota(jnp.int32, (rows, rows), 0) >= lo - base
-            all_scores = [scores_of(piece, head, rows, everything) for head in range(heads)]
-            for head in range(heads):
-                fold(piece, head, jnp.where(inside, all_scores[head], -1e30), False, everything)
+        for begin, met in ((0, first_lo < base + half), (half, first_lo >= base + half)):
+
+            @pl.when(needed & (last_lo > base) & met)
+            def _():
+                deep = rows - begin
+                inside = lax.broadcasted_iota(jnp.int32, (deep, rows), 0) >= lo - (base + begin)
+                all_scores = [scores_of(piece, head, deep, everything, begin) for head in range(heads)]
+                for head in range(heads):
+                    scores = jnp.where(inside, all_scores[head], -1e30)
+                    fold(piece, head, scores, False, everything, begin)
 
     for head in range(heads):
         result = acc_ref[head] / l_ref[head]

time: 167 us -> 165 us (0.988)
  transfers between devices with their start and end apart: 35 -> 35, of which waited for: 11 -> 11; matrix products, arithmetic and copies ran while one was open for 7% -> 7% of each run, Pallas kernels for 16% -> 15%
where the time goes in v1:
time: 165 us
  waiting for transfers between devices  76.3 us (46%)
  starting transfers between devices  46.6 us (28%)
  Pallas kernels  25 us (15%)
  matrix products  9.93 us (6%)
  local copies, waits for them, and re-layouts  3.44 us (2%)
  other arithmetic  3 us (2%)
    ppermute x4, waiting for transfers between devices, spread(): same.append(lax.ppermute(same[-1], 'seq', up))  26.2 us
    pallas_call x2, Pallas kernels, attend(): pl.pallas_call(functools.partial(attend_kernel, count, group, call // CAL...  25 us
    ppermute x6, waiting for transfers between devices, steps(): back[part] = lax.ppermute(back[part], 'seq', behind)  17.6 us
    ppermute x6, starting transfers between devices, spread(): across.append(lax.ppermute(same[-1], 'seq', pairs))  15 us
    ppermute x5, starting transfers between devices, reduced(): arrived = lax.ppermute(part, ('seq', 'head'), pairs)  11.9 us
    ppermute x5, waiting for transfers between devices, reduced(): arrived = lax.ppermute(part, ('seq', 'head'), pairs)  11.3 us
    ppermute x6, starting transfers between devices, steps(): forth[part] = lax.ppermute(forth[part], 'seq', ahead)  11.3 us
    ppermute x6, waiting for transfers between devices, spread(): across.append(lax.ppermute(same[-1], 'seq', pairs))  10.6 us
  transfers between devices with their start and end apart: 35, of which 11 were waited for; matrix products, arithmetic and copies ran while one was open for 7% of the time, Pallas kernels for 15%

profile of v1, /device:TPU:28, one launch (start us, length us, event | category | flops | bytes accessed | tf_op | source)
XLA Modules:
  0.0 164.8 jit_solution(9587444207162415529)
XLA Ops:
  0.0 1.3 collective-permute-start
  1.3 1.3 collective-permute-start.2
  2.6 1.3 collective-permute-start.7
  3.9 1.3 collective-permute-start.5
  5.2 6.0 %collective-permute-done.refs_1_ = bf16[512,256]{1,0:T(8,128)(2,1)S(1)} collective-permute-done((bf16[512,256]{1,0:T(8,128)(2,1)}, bf16[512,256]{1,0:T(8,128)(2,1)S(1)}, u32[]{:S(2)}, u32[]{:S(2)}) %collective-permute-start) | collective-permute-done | bytes 262176 | tf_op jit(solution)/shard_map/ppermute | solution.py:182
  11.2 1.9 %collective-permute-start.3 = (bf16[512,256]{1,0:T(8,128)(2,1)S(1)}, bf16[512,256]{1,0:T(8,128)(2,1)S(1)}, u32[]{:S(2)}, u32[]{:S(2)}) collective-permute-start(bf16[512,256]{1,0:T(8,128)(2,1)S(1)} %collective-permute-done.refs_1_), channel_id=1, source_target_pairs={{12,8},{8,12},{20,16},{16,20},{28,24},{24,28},{13,9},{9,13},{21,17... | collective-permute-start | bytes 786440 | tf_op jit(solution)/shard_map/ppermute | solution.py:188
  13.1 1.3 fusion.56
  14.4 1.3 collective-permute-start.1
  15.8 3.9 %collective-permute-start.8 = (bf16[512,256]{1,0:T(8,128)(2,1)S(1)}, bf16[512,256]{1,0:T(8,128)(2,1)S(1)}, u32[]{:S(2)}, u32[]{:S(2)}) collective-permute-start(bf16[512,256]{1,0:T(8,128)(2,1)S(1)} %collective-permute-done.5.refs_7_), channel_id=1, source_target_pairs={{12,8},{8,12},{20,16},{16,20},{28,24},{24,28},{13,9},{9,13},{21,17... | collective-permute-start | bytes 786440 | tf_op jit(solution)/shard_map/ppermute | solution.py:188
  19.7 0.7 copy-done.3
  20.4 2.7 %collective-permute-start.14 = (bf16[1024,256]{1,0:T(8,128)(2,1)S(1)}, bf16[1024,256]{1,0:T(8,128)(2,1)S(1)}, u32[]{:S(2)}, u32[]{:S(2)}) collective-permute-start(bf16[1024,256]{1,0:T(8,128)(2,1)S(1)} %get-tuple-element.11), channel_id=1, source_target_pairs={{0,8},{8,16},{16,24},{24,28},{28,20},{20,12},{12,4},{4,0},{1,9},{9... | collective-permute-start | bytes 1572872 | tf_op jit(solution)/shard_map/ppermute | solution.py:202
  23.1 0.7 collective-permute-done.3.refs_4_
  23.8 0.7 copy-done.6
  24.5 2.6 %collective-permute-start.10 = (bf16[1024,256]{1,0:T(8,128)(2,1)S(1)}, bf16[1024,256]{1,0:T(8,128)(2,1)S(1)}, u32[]{:S(2)}, u32[]{:S(2)}) collective-permute-start(bf16[1024,256]{1,0:T(8,128)(2,1)S(1)} %get-tuple-element.12), channel_id=1, source_target_pairs={{0,8},{8,16},{16,24},{24,28},{28,20},{20,12},{12,4},{4,0},{1,9},{9... | collective-permute-start | bytes 1572872 | tf_op jit(solution)/shard_map/ppermute | solution.py:202
  27.2 2.3 %collective-permute-done.8.refs_10_ = bf16[512,256]{1,0:T(8,128)(2,1)S(1)} collective-permute-done((bf16[512,256]{1,0:T(8,128)(2,1)S(1)}, bf16[512,256]{1,0:T(8,128)(2,1)S(1)}, u32[]{:S(2)}, u32[]{:S(2)}) %collective-permute-start.8) | collective-permute-done | bytes 262176 | tf_op jit(solution)/shard_map/ppermute | solution.py:188
  29.4 1.3 collective-permute-start.6
  30.7 20.1 %collective-permute-done.6.refs_8_ = bf16[512,256]{1,0:T(8,128)(2,1)S(1)} collective-permute-done((bf16[512,256]{1,0:T(8,128)(2,1)S(1)}, bf16[512,256]{1,0:T(8,128)(2,1)S(1)}, u32[]{:S(2)}, u32[]{:S(2)}) %collective-permute-start.6) | collective-permute-done | bytes 262176 | tf_op jit(solution)/shard_map/ppermute | solution.py:182
  50.8 4.6 %collective-permute-start.4 = (bf16[512,256]{1,0:T(8,128)(2,1)}, bf16[512,256]{1,0:T(8,128)(2,1)}, u32[]{:S(2)}, u32[]{:S(2)}) collective-permute-start(bf16[512,256]{1,0:T(8,128)(2,1)} %collective-permute-done.1.refs_2_), channel_id=1, source_target_pairs={{20,16},{28,24},{21,17},{29,25},{22,18},{30,26},{23,19},{31,27}} | collective-permute-start | bytes 786440 | tf_op jit(solution)/shard_map/ppermute | solution.py:188
  55.4 2.0 %collective-permute-start.9 = (bf16[512,256]{1,0:T(8,128)(2,1)S(1)}, bf16[512,256]{1,0:T(8,128)(2,1)}, u32[]{:S(2)}, u32[]{:S(2)}) collective-permute-start(bf16[512,256]{1,0:T(8,128)(2,1)S(1)} %collective-permute-done.6.refs_8_), channel_id=1, source_target_pairs={{20,16},{28,24},{21,17},{29,25},{22,18},{30,26},{23,19},{31,27}} | collective-permute-start | bytes 786440 | tf_op jit(solution)/shard_map/ppermute | solution.py:188
  57.4 2.0 %collective-permute-start.15 = (bf16[1024,256]{1,0:T(8,128)(2,1)S(1)}, bf16[1024,256]{1,0:T(8,128)(2,1)}, u32[]{:S(2)}, u32[]{:S(2)}) collective-permute-start(bf16[1024,256]{1,0:T(8,128)(2,1)S(1)} %collective-permute-done.14), channel_id=1, source_target_pairs={{0,8},{8,16},{16,24},{24,28},{28,20},{20,12},{12,4},{4,0},{1,9},{9... | collective-permute-start | bytes 1572872 | tf_op jit(solution)/shard_map/ppermute | solution.py:202
  59.5 2.2 %collective-permute-done.4.refs_5_ = bf16[512,256]{1,0:T(8,128)(2,1)} collective-permute-done((bf16[512,256]{1,0:T(8,128)(2,1)}, bf16[512,256]{1,0:T(8,128)(2,1)}, u32[]{:S(2)}, u32[]{:S(2)}) %collective-permute-start.4) | collective-permute-done | bytes 262176 | tf_op jit(solution)/shard_map/ppermute | solution.py:188
  61.7 5.5 %collective-permute-done.9.refs_11_ = bf16[512,256]{1,0:T(8,128)(2,1)} collective-permute-done((bf16[512,256]{1,0:T(8,128)(2,1)S(1)}, bf16[512,256]{1,0:T(8,128)(2,1)}, u32[]{:S(2)}, u32[]{:S(2)}) %collective-permute-start.9) | collective-permute-done | bytes 262176 | tf_op jit(solution)/shard_map/ppermute | solution.py:188
  67.2 12.4 %shard_map.55.refs_12_ = bf16[512,1024]{1,0:T(8,128)(2,1)} custom-call(s32[16]{0:T(128)} %lengths.3, bf16[512,1024]{1,0:T(8,128)(2,1)} %q_ref.3, bf16[512,256]{1,0:T(8,128)(2,1)} %refs_0_.3, bf16[512,256]{1,0:T(8,128)(2,1)} %copy-done.2, bf16[512,256]{1,0:T(8,128)(2,1)} %collective-permute-done.1.refs_2_, bf16[512,256]{1,0:T(8,128)(2,1)} %copy-done.3, ...), custom_call_target="tpu_custom_call" | custom-call | flops 3221225472 | bytes 2621440 | tf_op jit(solution)/shard_map/pallas_call | solution.py:142
  79.6 12.6 %shard_map.56 = bf16[512,1024]{1,0:T(8,128)(2,1)} custom-call(s32[16]{0:T(128)} %lengths.3, bf16[512,1024]{1,0:T(8,128)(2,1)} %q_ref.3, bf16[512,256]{1,0:T(8,128)(2,1)} %refs_0_.3, bf16[512,256]{1,0:T(8,128)(2,1)} %copy-done.2, bf16[512,256]{1,0:T(8,128)(2,1)} %collective-permute-done.1.refs_2_, ...), custom_call_target="tpu_custom_call", output_to_operand_aliasing={{}: (14, {})} | custom-call | flops 3221225472 | bytes 2621440 | tf_op jit(solution)/shard_map/pallas_call | solution.py:142
  92.2 1.9 %convolution_convert_fusion.10 = bf16[512,256]{1,0:T(8,128)(2,1)S(1)} fusion(bf16[512,1024]{1,0:T(8,128)(2,1)} %shard_map.56, bf16[1024,256]{1,0:T(8,128)(2,1)} %collective-permute-done.17, bf16[1024,256]{1,0:T(8,128)(2,1)} %collective-permute-done.15, pred[]{:T(512)S(6)} %eq.141), kind=kOutput, calls=%fused_computation.20 | convolution fusion | flops 268828672 | bytes 2359297 | tf_op jit(solution)/shard_map/dot_general | solution.py:233
  94.2 0.4 convolution_convert_fusion.11
  94.8 2.0 %collective-permute-start.21 = (bf16[1024,256]{1,0:T(8,128)(2,1)}, bf16[1024,256]{1,0:T(8,128)(2,1)S(1)}, u32[]{:S(2)}, u32[]{:S(2)}) collective-permute-start(bf16[1024,256]{1,0:T(8,128)(2,1)} %collective-permute-done.15), channel_id=1, source_target_pairs={{0,8},{8,16},{16,24},{24,28},{28,20},{20,12},{12,4},{4,0},{1,9},{9... | collective-permute-start | bytes 1572872 | tf_op jit(solution)/shard_map/ppermute | solution.py:202
  96.9 2.0 %collective-permute-start.20 = (bf16[1024,256]{1,0:T(8,128)(2,1)S(1)}, bf16[1024,256]{1,0:T(8,128)(2,1)S(1)}, u32[]{:S(2)}, u32[]{:S(2)}) collective-permute-start(bf16[1024,256]{1,0:T(8,128)(2,1)S(1)} %collective-permute-done.11), channel_id=1, source_target_pairs={{0,8},{8,16},{16,24},{24,28},{28,20},{20,12},{12,4},{4,0},{1,9},{9... | collective-permute-start | bytes 1572872 | tf_op jit(solution)/shard_map/ppermute | solution.py:202
  98.8 1.5 convolution_convert_fusion.12
  100.3 0.4 convolution_convert_fusion.13
  100.8 9.0 %collective-permute-done.25 = bf16[1024,256]{1,0:T(8,128)(2,1)S(1)} collective-permute-done((bf16[1024,256]{1,0:T(8,128)(2,1)}, bf16[1024,256]{1,0:T(8,128)(2,1)S(1)}, u32[]{:S(2)}, u32[]{:S(2)}) %collective-permute-start.25) | collective-permute-done | bytes 524320 | tf_op jit(solution)/shard_map/ppermute | solution.py:203
  109.9 2.1 %collective-permute-start.31 = (bf16[512,256]{1,0:T(8,128)(2,1)S(1)}, bf16[512,256]{1,0:T(8,128)(2,1)S(1)}, u32[]{:S(2)}, u32[]{:S(2)}) collective-permute-start(bf16[512,256]{1,0:T(8,128)(2,1)S(1)} %slice.37), channel_id=1, source_target_pairs={{0,8},{8,16},{16,24},{24,28},{28,20},{20,12},{12,4},{4,0},{1,9},{9... | collective-permute-start | bytes 786440 | tf_op jit(solution)/shard_map/ppermute | solution.py:208
  112.0 0.4 convolution_convert_fusion.2
  112.4 8.6 %collective-permute-done.24 = bf16[1024,256]{1,0:T(8,128)(2,1)S(1)} collective-permute-done((bf16[1024,256]{1,0:T(8,128)(2,1)S(1)}, bf16[1024,256]{1,0:T(8,128)(2,1)S(1)}, u32[]{:S(2)}, u32[]{:S(2)}) %collective-permute-start.24) | collective-permute-done | bytes 524320 | tf_op jit(solution)/shard_map/ppermute | solution.py:203
  121.0 0.4 convolution_convert_fusion.3
  121.6 0.1 add_convert_fusion.5
  121.8 3.4 %collective-permute-start.19 = (bf16[512,512]{1,0:T(8,128)(2,1)S(1)}, bf16[512,512]{1,0:T(8,128)(2,1)S(1)}, u32[]{:S(2)}, u32[]{:S(2)}) collective-permute-start(bf16[512,512]{1,0:T(8,128)(2,1)S(1)} %add_convert_fusion.5), channel_id=1, source_target_pairs={{0,2},{3,1},{4,6},{7,5},{9,11},{10,8},{13,15},{14,12},{17,19},{18,... | collective-permute-start | bytes 1572872 | tf_op jit(solution)/shard_map/ppermute | solution.py:258
  125.2 0.4 convolution_convert_fusion.6
  125.7 0.4 convolution_convert_fusion.7
  126.2 0.4 convolution_convert_fusion.4
  126.7 0.4 convolution_convert_fusion.8
  127.1 0.4 convolution_convert_fusion.5
  127.6 0.4 convolution_convert_fusion.9
  128.1 0.7 copy-done
  128.8 0.3 fusion.36
  129.1 0.3 fusion.4
  129.4 0.6 collective-permute-start.33
  130.0 0.3 fusion.38
  130.3 0.9 collective-permute-done.33
  131.2 0.3 fusion.3
  131.5 1.3 collective-permute-start.34
  132.8 9.7 %collective-permute-done.28 = bf16[1024,256]{1,0:T(8,128)(2,1)S(1)} collective-permute-done((bf16[1024,256]{1,0:T(8,128)(2,1)S(1)}, bf16[1024,256]{1,0:T(8,128)(2,1)S(1)}, u32[]{:S(2)}, u32[]{:S(2)}) %collective-permute-start.28) | collective-permute-done | bytes 524320 | tf_op jit(solution)/shard_map/ppermute | solution.py:207
  142.4 0.4 convolution_convert_fusion
  143.0 0.1 add_convert_fusion.1
  143.1 1.3 collective-permute-start.27
  144.6 4.6 %collective-permute-start.23 = (bf16[512,512]{1,0:T(8,128)(2,1)S(1)}, bf16[512,512]{1,0:T(8,128)(2,1)S(1)}, u32[]{:S(2)}, u32[]{:S(2)}) collective-permute-start(bf16[512,512]{1,0:T(8,128)(2,1)S(1)} %add_convert_fusion.3), channel_id=1, source_target_pairs={{0,2},{3,1},{5,7},{6,4},{8,10},{11,9},{13,15},{14,12},{17,19},{18,... | collective-permute-start | bytes 1572872 | tf_op jit(solution)/shard_map/ppermute | solution.py:258
  149.2 0.4 fusion.7
  149.6 1.3 collective-permute-start.30
  150.9 0.2 broadcast_select_fusion.5
  151.3 11.3 %collective-permute-done.30 = bf16[512,256]{1,0:T(8,128)(2,1)S(1)} collective-permute-done((bf16[512,256]{1,0:T(8,128)(2,1)S(1)}, bf16[512,256]{1,0:T(8,128)(2,1)S(1)}, u32[]{:S(2)}, u32[]{:S(2)}) %collective-permute-start.30) | collective-permute-done | bytes 262176 | tf_op jit(solution)/shard_map/ppermute | solution.py:258
  162.7 0.2 broadcast_select_fusion.1
  163.0 0.2 broadcast_select_fusion.3
  163.2 0.5 add_add_fusion.1
  163.7 1.2 add_add_fusion
  (60 shorter events, 1.2 us)
Async XLA Ops:
  0.0 11.2 %collective-permute-start = (bf16[512,256]{1,0:T(8,128)(2,1)}, bf16[512,256]{1,0:T(8,128)(2,1)S(1)}, u32[]{:S(2)}, u32[]{:S(2)}) collective-permute-start(bf16[512,256]{1,0:T(8,128)(2,1)} %refs_0_.3), channel_id=1, source_target_pairs={{0,8},{4,12},{8,16},{12,20},{16,24},{20,28},{1,9},{5,13},{9,17},{1... | collective-permute-start | bytes 786440 | tf_op jit(solution)/shard_map/ppermute | solution.py:182
  1.3 18.4 %collective-permute-start.2 = (bf16[512,256]{1,0:T(8,128)(2,1)}, bf16[512,256]{1,0:T(8,128)(2,1)S(1)}, u32[]{:S(2)}, u32[]{:S(2)}) collective-permute-start(bf16[512,256]{1,0:T(8,128)(2,1)} %refs_0_.3), channel_id=1, source_target_pairs={{0,4},{8,12},{16,20},{24,28},{1,5},{9,13},{17,21},{25,29},{2,6},{1... | collective-permute-start | bytes 786440 | tf_op jit(solution)/shard_map/ppermute | solution.py:188
  2.6 17.8 %collective-permute-start.7 = (bf16[512,256]{1,0:T(8,128)(2,1)}, bf16[512,256]{1,0:T(8,128)(2,1)S(1)}, u32[]{:S(2)}, u32[]{:S(2)}) collective-permute-start(bf16[512,256]{1,0:T(8,128)(2,1)} %refs_6_.3), channel_id=1, source_target_pairs={{0,4},{8,12},{16,20},{24,28},{1,5},{9,13},{17,21},{25,29},{2,6},{1... | collective-permute-start | bytes 786440 | tf_op jit(solution)/shard_map/ppermute | solution.py:188
  3.9 11.9 %collective-permute-start.5 = (bf16[512,256]{1,0:T(8,128)(2,1)}, bf16[512,256]{1,0:T(8,128)(2,1)S(1)}, u32[]{:S(2)}, u32[]{:S(2)}) collective-permute-start(bf16[512,256]{1,0:T(8,128)(2,1)} %refs_6_.3), channel_id=1, source_target_pairs={{0,8},{4,12},{8,16},{12,20},{16,24},{20,28},{1,9},{5,13},{9,17},{1... | collective-permute-start | bytes 786440 | tf_op jit(solution)/shard_map/ppermute | solution.py:182
  11.2 3.2 %copy-start.2 = (bf16[512,256]{1,0:T(8,128)(2,1)}, bf16[512,256]{1,0:T(8,128)(2,1)S(1)}, u32[]{:S(2)}) copy-start(bf16[512,256]{1,0:T(8,128)(2,1)S(1)} %collective-permute-done.refs_1_) | copy-start | bytes 786436
  11.2 12.6 %collective-permute-start.3 = (bf16[512,256]{1,0:T(8,128)(2,1)S(1)}, bf16[512,256]{1,0:T(8,128)(2,1)S(1)}, u32[]{:S(2)}, u32[]{:S(2)}) collective-permute-start(bf16[512,256]{1,0:T(8,128)(2,1)S(1)} %collective-permute-done.refs_1_), channel_id=1, source_target_pairs={{12,8},{8,12},{20,16},{16,20},{28,24},{24,28},{13,9},{9,13},{21,17... | collective-permute-start | bytes 786440 | tf_op jit(solution)/shard_map/ppermute | solution.py:188
  14.4 10.1 %collective-permute-start.1 = (bf16[512,256]{1,0:T(8,128)(2,1)S(1)}, bf16[512,256]{1,0:T(8,128)(2,1)}, u32[]{:S(2)}, u32[]{:S(2)}) collective-permute-start(bf16[512,256]{1,0:T(8,128)(2,1)S(1)} %collective-permute-done.refs_1_), channel_id=1, source_target_pairs={{8,16},{12,20},{16,24},{20,28},{9,17},{13,21},{17,25},{21,29},{10,... | collective-permute-start | bytes 786440 | tf_op jit(solution)/shard_map/ppermute | solution.py:182
  15.8 39.7 %copy-start.5 = (bf16[512,256]{1,0:T(8,128)(2,1)}, bf16[512,256]{1,0:T(8,128)(2,1)S(1)}, u32[]{:S(2)}) copy-start(bf16[512,256]{1,0:T(8,128)(2,1)S(1)} %collective-permute-done.5.refs_7_) | copy-start | bytes 786436
  15.8 13.7 %collective-permute-start.8 = (bf16[512,256]{1,0:T(8,128)(2,1)S(1)}, bf16[512,256]{1,0:T(8,128)(2,1)S(1)}, u32[]{:S(2)}, u32[]{:S(2)}) collective-permute-start(bf16[512,256]{1,0:T(8,128)(2,1)S(1)} %collective-permute-done.5.refs_7_), channel_id=1, source_target_pairs={{12,8},{8,12},{20,16},{16,20},{28,24},{24,28},{13,9},{9,13},{21,17... | collective-permute-start | bytes 786440 | tf_op jit(solution)/shard_map/ppermute | solution.py:188
  19.7 0.7 copy-start.3
  20.4 35.0 %collective-permute-start.16 = (bf16[1024,256]{1,0:T(8,128)(2,1)S(1)}, bf16[1024,256]{1,0:T(8,128)(2,1)S(1)}, u32[]{:S(2)}, u32[]{:S(2)}) collective-permute-start(bf16[1024,256]{1,0:T(8,128)(2,1)S(1)} %get-tuple-element.11), channel_id=1, source_target_pairs={{8,0},{16,8},{24,16},{28,24},{20,28},{12,20},{4,12},{0,4},{9,1},{1... | collective-permute-start | bytes 1572872 | tf_op jit(solution)/shard_map/ppermute | solution.py:203
  20.4 3.4 %copy-start.4 = (bf16[512,256]{1,0:T(8,128)(2,1)}, bf16[512,256]{1,0:T(8,128)(2,1)S(1)}, u32[]{:S(2)}) copy-start(bf16[512,256]{1,0:T(8,128)(2,1)S(1)} %collective-permute-done.7.refs_9_) | copy-start | bytes 786436
  20.4 37.0 %collective-permute-start.14 = (bf16[1024,256]{1,0:T(8,128)(2,1)S(1)}, bf16[1024,256]{1,0:T(8,128)(2,1)S(1)}, u32[]{:S(2)}, u32[]{:S(2)}) collective-permute-start(bf16[1024,256]{1,0:T(8,128)(2,1)S(1)} %get-tuple-element.11), channel_id=1, source_target_pairs={{0,8},{8,16},{16,24},{24,28},{28,20},{20,12},{12,4},{4,0},{1,9},{9... | collective-permute-start | bytes 1572872 | tf_op jit(solution)/shard_map/ppermute | solution.py:202
  23.8 0.7 copy-start.6
  24.5 32.9 %collective-permute-start.12 = (bf16[1024,256]{1,0:T(8,128)(2,1)S(1)}, bf16[1024,256]{1,0:T(8,128)(2,1)S(1)}, u32[]{:S(2)}, u32[]{:S(2)}) collective-permute-start(bf16[1024,256]{1,0:T(8,128)(2,1)S(1)} %get-tuple-element.12), channel_id=1, source_target_pairs={{8,0},{16,8},{24,16},{28,24},{20,28},{12,20},{4,12},{0,4},{9,1},{1... | collective-permute-start | bytes 1572872 | tf_op jit(solution)/shard_map/ppermute | solution.py:203
  24.5 34.9 %collective-permute-start.10 = (bf16[1024,256]{1,0:T(8,128)(2,1)S(1)}, bf16[1024,256]{1,0:T(8,128)(2,1)S(1)}, u32[]{:S(2)}, u32[]{:S(2)}) collective-permute-start(bf16[1024,256]{1,0:T(8,128)(2,1)S(1)} %get-tuple-element.12), channel_id=1, source_target_pairs={{0,8},{8,16},{16,24},{24,28},{28,20},{20,12},{12,4},{4,0},{1,9},{9... | collective-permute-start | bytes 1572872 | tf_op jit(solution)/shard_map/ppermute | solution.py:202
  29.4 28.0 %copy-start.7 = (bf16[512,256]{1,0:T(8,128)(2,1)}, bf16[512,256]{1,0:T(8,128)(2,1)S(1)}, u32[]{:S(2)}) copy-start(bf16[512,256]{1,0:T(8,128)(2,1)S(1)} %collective-permute-done.8.refs_10_) | copy-start | bytes 786436
  29.4 21.4 %collective-permute-start.6 = (bf16[512,256]{1,0:T(8,128)(2,1)S(1)}, bf16[512,256]{1,0:T(8,128)(2,1)S(1)}, u32[]{:S(2)}, u32[]{:S(2)}) collective-permute-start(bf16[512,256]{1,0:T(8,128)(2,1)S(1)} %collective-permute-done.5.refs_7_), channel_id=1, source_target_pairs={{8,16},{12,20},{16,24},{20,28},{9,17},{13,21},{17,25},{21,29},{10,... | collective-permute-start | bytes 786440 | tf_op jit(solution)/shard_map/ppermute | solution.py:182
  50.8 16.4 %copy-start.8 = (bf16[512,256]{1,0:T(8,128)(2,1)}, bf16[512,256]{1,0:T(8,128)(2,1)S(1)}, u32[]{:S(2)}) copy-start(bf16[512,256]{1,0:T(8,128)(2,1)S(1)} %collective-permute-done.6.refs_8_) | copy-start | bytes 786436
  50.8 10.9 %collective-permute-start.4 = (bf16[512,256]{1,0:T(8,128)(2,1)}, bf16[512,256]{1,0:T(8,128)(2,1)}, u32[]{:S(2)}, u32[]{:S(2)}) collective-permute-start(bf16[512,256]{1,0:T(8,128)(2,1)} %collective-permute-done.1.refs_2_), channel_id=1, source_target_pairs={{20,16},{28,24},{21,17},{29,25},{22,18},{30,26},{23,19},{31,27}} | collective-permute-start | bytes 786440 | tf_op jit(solution)/shard_map/ppermute | solution.py:188
  55.4 11.8 %collective-permute-start.9 = (bf16[512,256]{1,0:T(8,128)(2,1)S(1)}, bf16[512,256]{1,0:T(8,128)(2,1)}, u32[]{:S(2)}, u32[]{:S(2)}) collective-permute-start(bf16[512,256]{1,0:T(8,128)(2,1)S(1)} %collective-permute-done.6.refs_8_), channel_id=1, source_target_pairs={{20,16},{28,24},{21,17},{29,25},{22,18},{30,26},{23,19},{31,27}} | collective-permute-start | bytes 786440 | tf_op jit(solution)/shard_map/ppermute | solution.py:188
  57.4 34.8 %collective-permute-start.17 = (bf16[1024,256]{1,0:T(8,128)(2,1)S(1)}, bf16[1024,256]{1,0:T(8,128)(2,1)}, u32[]{:S(2)}, u32[]{:S(2)}) collective-permute-start(bf16[1024,256]{1,0:T(8,128)(2,1)S(1)} %collective-permute-done.16), channel_id=1, source_target_pairs={{8,0},{16,8},{24,16},{28,24},{20,28},{12,20},{4,12},{0,4},{9,1},{1... | collective-permute-start | bytes 1572872 | tf_op jit(solution)/shard_map/ppermute | solution.py:203
  57.4 34.8 %collective-permute-start.15 = (bf16[1024,256]{1,0:T(8,128)(2,1)S(1)}, bf16[1024,256]{1,0:T(8,128)(2,1)}, u32[]{:S(2)}, u32[]{:S(2)}) collective-permute-start(bf16[1024,256]{1,0:T(8,128)(2,1)S(1)} %collective-permute-done.14), channel_id=1, source_target_pairs={{0,8},{8,16},{16,24},{24,28},{28,20},{20,12},{12,4},{4,0},{1,9},{9... | collective-permute-start | bytes 1572872 | tf_op jit(solution)/shard_map/ppermute | solution.py:202
  59.5 34.7 %collective-permute-start.13 = (bf16[1024,256]{1,0:T(8,128)(2,1)S(1)}, bf16[1024,256]{1,0:T(8,128)(2,1)S(1)}, u32[]{:S(2)}, u32[]{:S(2)}) collective-permute-start(bf16[1024,256]{1,0:T(8,128)(2,1)S(1)} %collective-permute-done.12), channel_id=1, source_target_pairs={{8,0},{16,8},{24,16},{28,24},{20,28},{12,20},{4,12},{0,4},{9,1},{1... | collective-permute-start | bytes 1572872 | tf_op jit(solution)/shard_map/ppermute | solution.py:203
  61.7 32.5 %collective-permute-start.11 = (bf16[1024,256]{1,0:T(8,128)(2,1)S(1)}, bf16[1024,256]{1,0:T(8,128)(2,1)S(1)}, u32[]{:S(2)}, u32[]{:S(2)}) collective-permute-start(bf16[1024,256]{1,0:T(8,128)(2,1)S(1)} %collective-permute-done.10), channel_id=1, source_target_pairs={{0,8},{8,16},{16,24},{24,28},{28,20},{20,12},{12,4},{4,0},{1,9},{9... | collective-permute-start | bytes 1572872 | tf_op jit(solution)/shard_map/ppermute | solution.py:202
  92.2 1.9 %copy-start.1 = (bf16[512,1024]{1,0:T(8,128)(2,1)S(1)}, bf16[512,1024]{1,0:T(8,128)(2,1)}, u32[]{:S(2)}) copy-start(bf16[512,1024]{1,0:T(8,128)(2,1)} %shard_map.56) | copy-start | bytes 3145732
  94.7 26.9 %collective-permute-start.18 = (bf16[512,512]{1,0:T(8,128)(2,1)S(1)}, bf16[512,512]{1,0:T(8,128)(2,1)S(1)}, u32[]{:S(2)}, u32[]{:S(2)}) collective-permute-start(bf16[512,512]{1,0:T(8,128)(2,1)S(1)} %pad_maximum_fusion), channel_id=1, source_target_pairs={{0,1},{1,0},{2,3},{3,2},{4,5},{5,4},{6,7},{7,6},{8,9},{9,8},{10,11... | collective-permute-start | bytes 1572872 | tf_op jit(solution)/shard_map/ppermute | solution.py:246
  94.7 15.1 %collective-permute-start.25 = (bf16[1024,256]{1,0:T(8,128)(2,1)}, bf16[1024,256]{1,0:T(8,128)(2,1)S(1)}, u32[]{:S(2)}, u32[]{:S(2)}) collective-permute-start(bf16[1024,256]{1,0:T(8,128)(2,1)} %collective-permute-done.17), channel_id=1, source_target_pairs={{8,0},{16,8},{24,16},{28,24},{20,28},{12,20},{4,12},{0,4},{9,1},{1... | collective-permute-start | bytes 1572872 | tf_op jit(solution)/shard_map/ppermute | solution.py:203
  94.8 15.1 %collective-permute-start.21 = (bf16[1024,256]{1,0:T(8,128)(2,1)}, bf16[1024,256]{1,0:T(8,128)(2,1)S(1)}, u32[]{:S(2)}, u32[]{:S(2)}) collective-permute-start(bf16[1024,256]{1,0:T(8,128)(2,1)} %collective-permute-done.15), channel_id=1, source_target_pairs={{0,8},{8,16},{16,24},{24,28},{28,20},{20,12},{12,4},{4,0},{1,9},{9... | collective-permute-start | bytes 1572872 | tf_op jit(solution)/shard_map/ppermute | solution.py:202
  96.8 24.2 %collective-permute-start.24 = (bf16[1024,256]{1,0:T(8,128)(2,1)S(1)}, bf16[1024,256]{1,0:T(8,128)(2,1)S(1)}, u32[]{:S(2)}, u32[]{:S(2)}) collective-permute-start(bf16[1024,256]{1,0:T(8,128)(2,1)S(1)} %collective-permute-done.13), channel_id=1, source_target_pairs={{8,0},{16,8},{24,16},{28,24},{20,28},{12,20},{4,12},{0,4},{9,1},{1... | collective-permute-start | bytes 1572872 | tf_op jit(solution)/shard_map/ppermute | solution.py:203
  96.9 28.8 %collective-permute-start.20 = (bf16[1024,256]{1,0:T(8,128)(2,1)S(1)}, bf16[1024,256]{1,0:T(8,128)(2,1)S(1)}, u32[]{:S(2)}, u32[]{:S(2)}) collective-permute-start(bf16[1024,256]{1,0:T(8,128)(2,1)S(1)} %collective-permute-done.11), channel_id=1, source_target_pairs={{0,8},{8,16},{16,24},{24,28},{28,20},{20,12},{12,4},{4,0},{1,9},{9... | collective-permute-start | bytes 1572872 | tf_op jit(solution)/shard_map/ppermute | solution.py:202
  109.8 18.2 %collective-permute-start.32 = (bf16[512,256]{1,0:T(8,128)(2,1)S(1)}, bf16[512,256]{1,0:T(8,128)(2,1)S(1)}, u32[]{:S(2)}, u32[]{:S(2)}) collective-permute-start(bf16[512,256]{1,0:T(8,128)(2,1)S(1)} %slice.39), channel_id=1, source_target_pairs={{8,0},{16,8},{24,16},{28,24},{20,28},{12,20},{4,12},{0,4},{9,1},{1... | collective-permute-start | bytes 786440 | tf_op jit(solution)/shard_map/ppermute | solution.py:208
  109.9 19.2 %collective-permute-start.31 = (bf16[512,256]{1,0:T(8,128)(2,1)S(1)}, bf16[512,256]{1,0:T(8,128)(2,1)S(1)}, u32[]{:S(2)}, u32[]{:S(2)}) collective-permute-start(bf16[512,256]{1,0:T(8,128)(2,1)S(1)} %slice.37), channel_id=1, source_target_pairs={{0,8},{8,16},{16,24},{24,28},{28,20},{20,12},{12,4},{4,0},{1,9},{9... | collective-permute-start | bytes 786440 | tf_op jit(solution)/shard_map/ppermute | solution.py:208
  121.5 21.4 %collective-permute-start.26 = (bf16[512,512]{1,0:T(8,128)(2,1)S(1)}, bf16[512,512]{1,0:T(8,128)(2,1)S(1)}, u32[]{:S(2)}, u32[]{:S(2)}) collective-permute-start(bf16[512,512]{1,0:T(8,128)(2,1)S(1)} %pad_maximum_fusion.2), channel_id=1, source_target_pairs={{0,1},{1,0},{2,3},{3,2},{4,5},{5,4},{6,7},{7,6},{8,9},{9,8},{10,11... | collective-permute-start | bytes 1572872 | tf_op jit(solution)/shard_map/ppermute | solution.py:246
  121.8 29.2 %collective-permute-start.19 = (bf16[512,512]{1,0:T(8,128)(2,1)S(1)}, bf16[512,512]{1,0:T(8,128)(2,1)S(1)}, u32[]{:S(2)}, u32[]{:S(2)}) collective-permute-start(bf16[512,512]{1,0:T(8,128)(2,1)S(1)} %add_convert_fusion.5), channel_id=1, source_target_pairs={{0,2},{3,1},{4,6},{7,5},{9,11},{10,8},{13,15},{14,12},{17,19},{18,... | collective-permute-start | bytes 1572872 | tf_op jit(solution)/shard_map/ppermute | solution.py:258
  126.1 18.3 %collective-permute-start.22 = (bf16[512,512]{1,0:T(8,128)(2,1)S(1)}, bf16[512,512]{1,0:T(8,128)(2,1)S(1)}, u32[]{:S(2)}, u32[]{:S(2)}) collective-permute-start(bf16[512,512]{1,0:T(8,128)(2,1)S(1)} %pad_maximum_fusion.1), channel_id=1, source_target_pairs={{0,1},{1,0},{2,3},{3,2},{4,5},{5,4},{6,7},{7,6},{8,9},{9,8},{10,11... | collective-permute-start | bytes 1572872 | tf_op jit(solution)/shard_map/ppermute | solution.py:246
  127.6 1.2 copy-start
  128.1 14.4 %collective-permute-start.28 = (bf16[1024,256]{1,0:T(8,128)(2,1)S(1)}, bf16[1024,256]{1,0:T(8,128)(2,1)S(1)}, u32[]{:S(2)}, u32[]{:S(2)}) collective-permute-start(bf16[1024,256]{1,0:T(8,128)(2,1)S(1)} %collective-permute-done.20), channel_id=1, source_target_pairs={{0,8},{8,16},{16,24},{24,28},{28,20},{20,12},{12,4},{4,0},{1,9},{9... | collective-permute-start | bytes 1572872 | tf_op jit(solution)/shard_map/ppermute | solution.py:207
  129.4 1.7 %collective-permute-start.33 = (bf16[512,256]{1,0:T(8,128)(2,1)S(1)}, bf16[512,256]{1,0:T(8,128)(2,1)S(1)}, u32[]{:S(2)}, u32[]{:S(2)}) collective-permute-start(bf16[512,256]{1,0:T(8,128)(2,1)S(1)} %fusion.4), channel_id=1, source_target_pairs={{0,1},{1,0},{2,3},{3,2},{4,5},{5,4},{6,7},{7,6},{8,9},{9,8},{10,11... | collective-permute-start | bytes 786440 | tf_op jit(solution)/shard_map/ppermute | solution.py:246
  131.5 19.7 %collective-permute-start.34 = (bf16[512,256]{1,0:T(8,128)(2,1)S(1)}, bf16[512,256]{1,0:T(8,128)(2,1)S(1)}, u32[]{:S(2)}, u32[]{:S(2)}) collective-permute-start(bf16[512,256]{1,0:T(8,128)(2,1)S(1)} %fusion.3), channel_id=1, source_target_pairs={{1,3},{2,0},{5,7},{6,4},{8,10},{11,9},{12,14},{15,13},{16,18},{19,... | collective-permute-start | bytes 786440 | tf_op jit(solution)/shard_map/ppermute | solution.py:258
  142.9 6.3 %collective-permute-start.29 = (bf16[512,256]{1,0:T(8,128)(2,1)S(1)}, bf16[512,256]{1,0:T(8,128)(2,1)S(1)}, u32[]{:S(2)}, u32[]{:S(2)}) collective-permute-start(bf16[512,256]{1,0:T(8,128)(2,1)S(1)} %convolution_convert_fusion), channel_id=1, source_target_pairs={{0,1},{1,0},{2,3},{3,2},{4,5},{5,4},{6,7},{7,6},{8,9},{9,8},{10,11... | collective-permute-start | bytes 786440 | tf_op jit(solution)/shard_map/ppermute | solution.py:246
  143.1 19.6 %collective-permute-start.27 = (bf16[512,512]{1,0:T(8,128)(2,1)S(1)}, bf16[512,512]{1,0:T(8,128)(2,1)S(1)}, u32[]{:S(2)}, u32[]{:S(2)}) collective-permute-start(bf16[512,512]{1,0:T(8,128)(2,1)S(1)} %add_convert_fusion.1), channel_id=1, source_target_pairs={{1,3},{2,0},{4,6},{7,5},{9,11},{10,8},{12,14},{15,13},{16,18},{19,... | collective-permute-start | bytes 1572872 | tf_op jit(solution)/shard_map/ppermute | solution.py:258
  144.6 18.4 %collective-permute-start.23 = (bf16[512,512]{1,0:T(8,128)(2,1)S(1)}, bf16[512,512]{1,0:T(8,128)(2,1)S(1)}, u32[]{:S(2)}, u32[]{:S(2)}) collective-permute-start(bf16[512,512]{1,0:T(8,128)(2,1)S(1)} %add_convert_fusion.3), channel_id=1, source_target_pairs={{0,2},{3,1},{5,7},{6,4},{8,10},{11,9},{13,15},{14,12},{17,19},{18,... | collective-permute-start | bytes 1572872 | tf_op jit(solution)/shard_map/ppermute | solution.py:258
  149.6 13.0 %collective-permute-start.30 = (bf16[512,256]{1,0:T(8,128)(2,1)S(1)}, bf16[512,256]{1,0:T(8,128)(2,1)S(1)}, u32[]{:S(2)}, u32[]{:S(2)}) collective-permute-start(bf16[512,256]{1,0:T(8,128)(2,1)S(1)} %fusion.7), channel_id=1, source_target_pairs={{1,3},{2,0},{5,7},{6,4},{8,10},{11,9},{12,14},{15,13},{16,18},{19,... | collective-permute-start | bytes 786440 | tf_op jit(solution)/shard_map/ppermute | solution.py:258
